TPU v7x, 512 devices: a whole 4x4x16 slice. The times are simulated.
512 devices in a mesh: box: 16 (over x, y_hi, core), sib: 2 (over y_lo), grp: 16 (over z).
Axes of the slice: x: 4, y: 4 (y_hi: 2, y_lo: 2; y = y_hi * 2 + y_lo), z: 16, core: 2. Of those that a mesh axis runs over, the one named last changes fastest.
Arguments:
- interface_maps: float32 [2, 32, 1024, 1024], P('sib', 'box', 'grp'), parts along dimension 1, may hold values from -1 to 1
- pivot_inverses: float32 [2, 32, 512, 512], P('sib', 'box', None, 'grp'), parts along dimension 1, may hold values from -1 to 5
- exterior_coupling: float32 [32, 1024, 5120], P('box', 'sib', 'grp'), parts along dimension 0, may hold values from -1 to 1
- face_blocks: int32 [32, 8], P('box'), parts along dimension 0, may hold values from 0 to 7, each once within a row
Outputs:
- interface_schur: float32 [32, 1024, 1024], P('box', 'sib', 'grp'), parts along dimension 0
- exterior_update: float32 [32, 1024, 5120], P('box', 'sib', 'grp'), parts along dimension 0
- multipliers: float32 [32, 1024, 1024], P('box', 'grp', 'sib'), parts along dimension 0
There are 16 independent parts, one for each index of `box`. A program takes and returns all parts, laid end to end along the dimension named above; each array names one. Nothing has to cross between parts.
Inputs may be any that keep to these rules, and one draw needn't show every extreme that they name: `face_blocks`: each row is an ordering of the 8 blocks of one child: row 0 for the first child, row 1 for the second.
All inputs are finite; a program needn't handle non-finite values.
Results may differ from a plain program's by a relative error of at most 0.0001.
Values sent between devices are 32-bit elements; how exact they have to be, the bound alone decides.
A program may use at most 128 MiB of HBM per device.

v0:
```python
import jax
import jax.numpy as jnp
from jax import lax
from jax.sharding import PartitionSpec as P


def partner(block, axis, bit):
    count = lax.axis_size(axis)
    route = []
    for low in range(count):
        high = low | 1 << bit
        if high != low and high < count:
            route += [(low, high), (high, low)]
    return lax.ppermute(block, axis, route)


def in_blocks(shard, dim, count):
    dims = shard.shape
    pieces = shard.reshape(*dims[:dim], count, dims[dim] // count, *dims[dim + 1 :])
    return jnp.moveaxis(pieces, dim, 0)


def summed_on_arrival(shard, axis, dim):
    pieces = in_blocks(shard, dim, lax.axis_size(axis))
    arrived = lax.all_to_all(pieces, axis, split_axis=0, concat_axis=0, tiled=True)
    return arrived.sum(axis=0)


def in_one_piece(arrays, axis, dim, along):
    ends, at = ([], 0)
    for a in arrays[:-1]:
        at += a.shape[along]
        ends.append(at)
    both = jnp.concatenate(arrays, axis=along)
    return tuple(jnp.split(summed_on_arrival(both, axis, dim), ends, axis=along))


def complex_dot(left_side, right_side):

    def product(first_part, second_part):
        return jnp.dot(
            first_part,
            second_part,
            precision=lax.Precision.HIGHEST,
            preferred_element_type=jnp.float32,
        )

    real_part = product(left_side[0], right_side[0]) - product(left_side[1], right_side[1])
    imag_part = product(left_side[0], right_side[1]) + product(left_side[1], right_side[0])
    return jnp.stack([real_part, imag_part])


def block_sources(face_blocks):
    alpha_order = face_blocks[0]
    beta_order = face_blocks[1]
    slots = jnp.arange(face_blocks.shape[1], dtype=jnp.int32)
    beta_match = (beta_order[:, None] == slots[None, :]).astype(jnp.int32)
    alpha_match = (alpha_order[:, None] == slots[None, :]).astype(jnp.int32)
    to_beta = jnp.sum(beta_match * alpha_order[:, None], axis=0)
    to_alpha = jnp.sum(alpha_match * beta_order[:, None], axis=0)
    return (to_beta, to_alpha)


def reorder(matrix, source):
    blocks = source.shape[0]
    grouped = matrix.reshape(matrix.shape[0], blocks, matrix.shape[1] // blocks, matrix.shape[2])
    return jnp.take(grouped, source, axis=1).reshape(matrix.shape)


def per_device(interface_maps, pivot_inverses, exterior_coupling, face_blocks):
    own_rows = interface_maps[0]
    partner_rows = partner(own_rows, "sib", 0)
    sibling = lax.axis_index("sib")
    member = lax.axis_index("grp")
    alpha_rows = jnp.where(sibling == 0, own_rows, partner_rows)
    beta_rows = jnp.where(sibling == 0, partner_rows, own_rows)
    local_rows = own_rows.shape[1]
    order_size = own_rows.shape[2]
    panel_width = pivot_inverses.shape[2]
    half_rows = order_size // 2
    to_beta, to_alpha = block_sources(face_blocks)
    panel_section = lax.dynamic_slice_in_dim(alpha_rows, sibling * panel_width, panel_width, 2)
    raw_multipliers = complex_dot(
        panel_section, lax.all_gather(pivot_inverses, "grp", axis=3, tiled=True)[0]
    )
    beta_cols = lax.all_to_all(beta_rows, "grp", split_axis=2, concat_axis=1, tiled=True)
    beta_perm = reorder(beta_cols, to_alpha)
    local_cols = beta_perm.shape[2]
    beta_panel = lax.dynamic_slice_in_dim(beta_perm, sibling * panel_width, panel_width, 1)
    piece = lax.all_gather(raw_multipliers, "grp", axis=1, tiled=True)
    joined = jnp.concatenate(
        [piece, -complex_dot(piece, beta_panel), complex_dot(piece, exterior_coupling)], axis=2
    )
    joined = reorder(joined, to_beta)
    multipliers = lax.dynamic_slice_in_dim(
        joined[:, :, :panel_width], member * local_rows, local_rows, 1
    )
    partial_schur = joined[:, :, panel_width : panel_width + local_cols]
    partial_exterior = joined[:, :, panel_width + local_cols :]
    summed_schur, exterior_update = in_one_piece((partial_schur, partial_exterior), "sib", 1, 2)
    row_index = sibling * half_rows + jnp.arange(half_rows, dtype=jnp.int32)
    col_index = member * local_cols + jnp.arange(local_cols, dtype=jnp.int32)
    identity_real = (row_index[:, None] == col_index[None, :]).astype(jnp.float32)
    identity_block = jnp.stack([identity_real, jnp.zeros_like(identity_real)])
    interface_schur = identity_block + summed_schur
    return (interface_schur, exterior_update, multipliers)


def solution(mesh):
    in_specs = (
        P("sib", "box", "grp", None),
        P("sib", "box", None, "grp"),
        P("box", "sib", "grp"),
        P("box", None),
    )
    out_specs = (P("box", "sib", "grp"), P("box", "sib", "grp"), P("box", "grp", "sib"))
    return jax.shard_map(
        per_device, mesh=mesh, in_specs=in_specs, out_specs=out_specs, check_vma=False
    )
```

profile of v0, /device:TPU:4, one launch (start us, length us, event | category | flops | bytes accessed | tf_op | source)
XLA Modules:
  0.0 277.3 jit_solution(12519139690456995614)
XLA Ops:
  7.2 0.7 all-gather.3.cloned.1.call-update
  7.9 3.5 %collective-permute-start = (f32[2,64,1024]{2,1,0:T(8,128)}, f32[2,64,1024]{2,1,0:T(8,128)S(1)}, u32[]{:S(2)}, u32[]{:S(2)}) collective-permute-start(f32[2,64,1024]{2,1,0:T(8,128)} %bitcast.121), channel_id=1, source_target_pairs={{0,16},{16,0},{1,17},{17,1},{2,18},{18,2},{3,19},{19,3},{4,20},{20... | collective-permute-start | bytes 1572872 | tf_op jit(solution)/shard_map/ppermute | solution.py:14
  11.4 12.3 %collective-permute-done = f32[2,64,1024]{2,1,0:T(8,128)S(1)} collective-permute-done((f32[2,64,1024]{2,1,0:T(8,128)}, f32[2,64,1024]{2,1,0:T(8,128)S(1)}, u32[]{:S(2)}, u32[]{:S(2)}) %collective-permute-start) | collective-permute-done | bytes 524320 | tf_op jit(solution)/shard_map/ppermute | solution.py:14
  23.7 1.0 dynamic-slice_select_fusion.1
  24.7 62.4 %all-gather.3.cloned.1.call-done = f32[1,2,512,512]{2,3,1,0:T(8,128)} async-done(((f32[1,2,512,32]{2,3,1,0:T(8,128)}), f32[1,2,512,512]{2,3,1,0:T(8,128)}) %all-gather.3.cloned.1.call-update) | async-done | bytes 2097168 | tf_op jit(solution)/shard_map/all_gather | solution.py:84
  87.1 2.5 fusion.19
  89.6 2.3 fusion.18
  91.9 1.1 fusion.17
  93.0 1.1 fusion.16
  94.2 0.7 pad_maximum_fusion.2
  95.0 0.6 copy.106
  95.6 1.9 reshape.137
  97.5 8.0 %all-to-all-start = ((f32[16,1,8192]{2,1,0:T(1,128)}), f32[16,1,8192]{2,1,0:T(1,128)S(1)}, u32[]{:S(2)}, u32[]{:S(2)}) async-start(f32[16,1,8192]{2,1,0:T(1,128)} %reshape.137), calls=%async_computation | async-start | bytes 1048576 | tf_op jit(solution)/shard_map/all_to_all | solution.py:86
  105.9 24.2 %all-to-all-done = f32[16,1,8192]{2,1,0:T(1,128)S(1)} async-done(((f32[16,1,8192]{2,1,0:T(1,128)}), f32[16,1,8192]{2,1,0:T(1,128)S(1)}, u32[]{:S(2)}, u32[]{:S(2)}) %all-to-all-start) | async-done | bytes 524320 | tf_op jit(solution)/shard_map/all_to_all | solution.py:86
  130.0 0.5 broadcast.132
  130.6 1.9 reduce
  132.5 0.8 reshape.138
  133.2 0.6 copy.123
  133.8 0.2 reshape.118
  134.2 0.6 gather_fusion
  134.8 43.9 %all-gather.5.cloned.1.call-done = f32[2,1024,512]{2,1,0:T(8,128)} async-done(((f32[2,64,512]{2,1,0:T(8,128)}), f32[2,1024,512]{2,1,0:T(8,128)}) %all-gather.5.cloned.1.call-update) | async-done | bytes 4194320 | tf_op jit(solution)/shard_map/all_gather | solution.py:90
  178.7 3.9 %fusion.3 = f32[1024,64]{0,1:T(8,128)S(1)} fusion(f32[2,1024,512]{2,1,0:T(8,128)} %all-gather.5.cloned.1.call-done, f32[2,512,64]{1,2,0:T(8,128)S(1)} %dynamic-slice_select_fusion), kind=kOutput, calls=%fused_computation.10 | convolution fusion | flops 402653184 | bytes 2490368 | tf_op jit(solution)/shard_map/dot_general | solution.py:41
  182.6 3.7 %fusion.2 = f32[1024,64]{0,1:T(8,128)S(1)} fusion(f32[2,1024,512]{2,1,0:T(8,128)} %all-gather.5.cloned.1.call-done, f32[2,512,64]{1,2,0:T(8,128)S(1)} %dynamic-slice_select_fusion), kind=kOutput, calls=%fused_computation.9 | convolution fusion | flops 402653184 | bytes 2490368 | tf_op jit(solution)/shard_map/dot_general | solution.py:41
  186.3 2.2 fusion.13
  188.5 2.2 fusion.15
  190.7 1.3 copy.110
  192.0 4.3 %fusion.1 = f32[1024,320]{0,1:T(8,128)S(1)} fusion(f32[2,1024,512]{2,1,0:T(8,128)} %all-gather.5.cloned.1.call-done, f32[2,512,320]{1,2,0:T(8,128)S(1)} %copy-done.4), kind=kOutput, calls=%fused_computation.8 | convolution fusion | flops 2013265920 | bytes 4063232 | tf_op jit(solution)/shard_map/dot_general | solution.py:41
  196.3 3.9 %fusion = f32[1024,320]{0,1:T(8,128)S(1)} fusion(f32[2,1024,512]{2,1,0:T(8,128)} %all-gather.5.cloned.1.call-done, f32[2,512,320]{1,2,0:T(8,128)S(1)} %copy-done.4), kind=kOutput, calls=%fused_computation.7 | convolution fusion | flops 2013265920 | bytes 4063232 | tf_op jit(solution)/shard_map/dot_general | solution.py:41
  200.3 2.4 fusion.9
  202.7 2.4 fusion.11
  205.1 1.7 pad_maximum_fusion.1
  206.8 2.3 copy.111
  209.1 5.5 %pad_maximum_fusion = f32[2,1024,896]{2,1,0:T(8,128)} fusion(f32[2,1024,320]{2,1,0:T(8,128)S(1)} %copy.111, f32[2,1024,64]{2,1,0:T(8,128)} %copy.110, f32[2,1024,512]{2,1,0:T(8,128)} %all-gather.5.cloned.1.call-done), kind=kLoop, calls=%fused_computation.2 | loop fusion | flops 3670016 | bytes 14680064 | tf_op jit(solution)/shard_map/concatenate | solution.py:91
  214.6 7.1 %gather_fusion.1 = f32[8,2,128,896]{3,2,1,0:T(8,128)} fusion(f32[2,8,128,896]{3,2,1,0:T(8,128)} %bitcast.116, s32[1024]{0:T(1024)S(1)} %pad_clamp_fusion), kind=kCustom, calls=%fused_computation.1 | custom fusion | bytes 14680096 | tf_op jit(solution)/shard_map/jit(_take)/gather | solution.py:67
  221.7 3.8 %copy.112 = f32[2,8,128,896]{3,2,1,0:T(8,128)S(1)} copy(f32[2,8,128,896]{3,2,0,1:T(8,128)} %bitcast.115) | data formatting | bytes 14680064 | tf_op jit(solution)/shard_map/jit(_take)/gather | solution.py:67
  225.5 0.6 bitcast_select_fusion
  226.0 2.9 %copy-done.2 = f32[2,1024,896]{2,1,0:T(8,128)} copy-done((f32[2,1024,896]{2,1,0:T(8,128)}, f32[2,1024,896]{2,1,0:T(8,128)S(1)}, u32[]{:S(2)}) %copy-start.2) | copy-done | bytes 7340056
  229.0 0.2 concatenate.8
  229.2 1.9 copy.113
  231.1 3.9 %all-to-all-start.1 = ((f32[2,2,512,384]{3,2,1,0:T(8,128)}), f32[2,2,512,384]{3,2,1,0:T(8,128)S(1)}, u32[]{:S(2)}, u32[]{:S(2)}) async-start(f32[2,2,512,384]{3,2,1,0:T(8,128)} %copy.113), calls=%async_computation.1 | async-start | bytes 6291456 | tf_op jit(solution)/shard_map/all_to_all | solution.py:25
  235.2 2.2 slice-done
  237.4 0.7 constant_dynamic-slice_fusion
  238.1 25.5 %all-to-all-done.1 = f32[2,2,512,384]{3,2,1,0:T(8,128)S(1)} async-done(((f32[2,2,512,384]{3,2,1,0:T(8,128)}), f32[2,2,512,384]{3,2,1,0:T(8,128)S(1)}, u32[]{:S(2)}, u32[]{:S(2)}) %all-to-all-start.1) | async-done | bytes 3145760 | tf_op jit(solution)/shard_map/all_to_all | solution.py:25
  263.6 1.5 reduce_sum.35
  265.1 1.9 split.9
  267.0 1.5 copy.116
  268.5 1.1 slice_add_fusion
  269.6 0.9 copy.115
  (35 shorter events, 0.9 us)
Async XLA Ops:
  7.2 79.9 %all-gather.3.cloned.1.call-start = ((), (), s32[]{:S(2)}) async-start(), calls=%async_computation.2 | async-start | bytes 2228224 | tf_op jit(solution)/shard_map/all_gather | solution.py:84
  7.9 170.8 %all-gather.5.cloned.1.call-start = ((), (), s32[]{:S(2)}) async-start(), calls=%async_computation.3 | async-start | bytes 4456448 | tf_op jit(solution)/shard_map/all_gather | solution.py:90
  7.9 15.8 %collective-permute-start = (f32[2,64,1024]{2,1,0:T(8,128)}, f32[2,64,1024]{2,1,0:T(8,128)S(1)}, u32[]{:S(2)}, u32[]{:S(2)}) collective-permute-start(f32[2,64,1024]{2,1,0:T(8,128)} %bitcast.121), channel_id=1, source_target_pairs={{0,16},{16,0},{1,17},{17,1},{2,18},{18,2},{3,19},{19,3},{4,20},{20... | collective-permute-start | bytes 1572872 | tf_op jit(solution)/shard_map/ppermute | solution.py:14
  87.1 4.8 %copy-start.3 = (f32[1,2,512,512]{2,3,1,0:T(8,128)S(1)}, f32[1,2,512,512]{2,3,1,0:T(8,128)}, u32[]{:S(2)}) copy-start(f32[1,2,512,512]{2,3,1,0:T(8,128)} %all-gather.3.cloned.1.call-done) | copy-start | bytes 6291460
  91.9 3.0 %copy-start.5 = (f32[1,2,64,1024]{3,2,1,0:T(8,128)S(1)}, f32[1,2,64,1024]{3,2,1,0:T(8,128)}, u32[]{:S(2)}) copy-start(f32[1,2,64,1024]{3,2,1,0:T(8,128)} %param.4) | copy-start | bytes 1572868
  95.0 10.5 %copy-start.6 = (s32[2,8]{1,0:T(2,128)S(1)}, s32[2,8]{1,0:T(2,128)}, u32[]{:S(2)}) copy-start(s32[2,8]{1,0:T(2,128)} %param.7) | copy-start | bytes 196
  97.5 32.6 %all-to-all-start = ((f32[16,1,8192]{2,1,0:T(1,128)}), f32[16,1,8192]{2,1,0:T(1,128)S(1)}, u32[]{:S(2)}, u32[]{:S(2)}) async-start(f32[16,1,8192]{2,1,0:T(1,128)} %reshape.137), calls=%async_computation | async-start | bytes 1048576 | tf_op jit(solution)/shard_map/all_to_all | solution.py:86
  178.7 7.6 %copy-start = (f32[2,1024,512]{2,1,0:T(8,128)S(1)}, f32[2,1024,512]{2,1,0:T(8,128)}, u32[]{:S(2)}) copy-start(f32[2,1024,512]{2,1,0:T(8,128)} %all-gather.5.cloned.1.call-done) | copy-start | bytes 12582916
  188.5 3.5 %copy-start.4 = (f32[2,512,320]{1,2,0:T(8,128)S(1)}, f32[2,512,320]{1,2,0:T(8,128)}, u32[]{:S(2)}) copy-start(f32[2,512,320]{1,2,0:T(8,128)} %param.6) | copy-start | bytes 3932164
  192.0 8.3 %copy-start.1 = (f32[2,1024,512]{2,1,0:T(8,128)S(1)}, f32[2,1024,512]{2,1,0:T(8,128)}, u32[]{:S(2)}) copy-start(f32[2,1024,512]{2,1,0:T(8,128)} %all-gather.5.cloned.1.call-done) | copy-start | bytes 12582916
  226.0 2.9 %copy-start.2 = (f32[2,1024,896]{2,1,0:T(8,128)}, f32[2,1024,896]{2,1,0:T(8,128)S(1)}, u32[]{:S(2)}) copy-start(f32[2,1024,896]{2,1,0:T(8,128)S(1)} %bitcast_select_fusion) | copy-start | bytes 22020100
  231.1 32.5 %all-to-all-start.1 = ((f32[2,2,512,384]{3,2,1,0:T(8,128)}), f32[2,2,512,384]{3,2,1,0:T(8,128)S(1)}, u32[]{:S(2)}, u32[]{:S(2)}) async-start(f32[2,2,512,384]{3,2,1,0:T(8,128)} %copy.113), calls=%async_computation.1 | async-start | bytes 6291456 | tf_op jit(solution)/shard_map/all_to_all | solution.py:25
  235.2 2.2 slice-start
Sparse Core Ops, SparseCore 0:
  10.1 76.9 all-gather.2
  95.0 83.6 all-gather.4
where the time goes:
time: 278 us; the launch traced here: 277 us
  waiting for transfers between devices  169 us (61%)
  local copies, waits for them, and re-layouts  32.3 us (12%)
  matrix products  32 us (12%)
  starting transfers between devices  15.5 us (6%)
  between operations  14.4 us (5%)
  other arithmetic  14.3 us (5%)
    all_gather x1, waiting for transfers between devices, per_device(): lax.all_gather(pivot_inverses, 'grp', axis=3, tiled=True)[0]  62.4 us
    all_gather x1, waiting for transfers between devices, per_device(): piece = lax.all_gather(raw_multipliers, 'grp', axis=1, tiled=True)  43.9 us
    dot_general x12, matrix products, product(): jnp.dot(first_part, second_part, precision=lax.Precision.HIGHEST, preferr...  32 us
    all_to_all x1, waiting for transfers between devices, summed_on_arrival(): lax.all_to_all(pieces, axis, split_axis=0, concat_axis=0, tiled=True)  25.5 us
    all_to_all x1, waiting for transfers between devices, per_device(): lax.all_to_all(beta_rows, 'grp', split_axis=2, concat_axis=1, tiled=True)  24.2 us
    ppermute x1, waiting for transfers between devices, partner(): return lax.ppermute(block, axis, route)  12.3 us
    gather x4, local copies, waits for them, and re-layouts, reorder(): return jnp.take(grouped, source, axis=1).reshape(matrix.shape)  11.5 us
    unnamed x18, local copies, waits for them, and re-layouts  8.03 us
  transfers between devices with their start and end apart: 5, of which 5 were waited for; matrix products, arithmetic and copies ran while one was open for 3% of the time, Pallas kernels for 0%

commit v1 on v0

--- a/solution.py
+++ b/solution.py
@@ -2,6 +2,7 @@
 import jax.numpy as jnp
 from jax import lax
 from jax.sharding import PartitionSpec as P
+from jax.lax import all_to_all, axis_size
 
 
 def partner(block, axis, bit):
@@ -68,6 +69,18 @@
 
 
 def per_device(interface_maps, pivot_inverses, exterior_coupling, face_blocks):
+
+    def _finish_screen(bus_axis, which_dim, vec):
+        n_shards = axis_size(bus_axis)
+        stack_in = list(map(lambda nth: n_shards if nth == which_dim else 1, range(vec.ndim)))
+        return all_to_all(
+            jnp.tile(vec, stack_in),
+            bus_axis,
+            concat_axis=which_dim,
+            tiled=True,
+            split_axis=which_dim,
+        )
+
     own_rows = interface_maps[0]
     partner_rows = partner(own_rows, "sib", 0)
     sibling = lax.axis_index("sib")
@@ -87,7 +100,7 @@
     beta_perm = reorder(beta_cols, to_alpha)
     local_cols = beta_perm.shape[2]
     beta_panel = lax.dynamic_slice_in_dim(beta_perm, sibling * panel_width, panel_width, 1)
-    piece = lax.all_gather(raw_multipliers, "grp", axis=1, tiled=True)
+    piece = _finish_screen("grp", 1, raw_multipliers)
     joined = jnp.concatenate(
         [piece, -complex_dot(piece, beta_panel), complex_dot(piece, exterior_coupling)], axis=2
     )

time: 278 us -> 414 us (1.49)
  the two profiles are of different devices: /device:TPU:4 before, /device:TPU:6 now
where the time goes in v1:
time: 414 us; the launch traced here: 413 us
  waiting for transfers between devices  274 us (66%)
  local copies, waits for them, and re-layouts  48.5 us (12%)
  starting transfers between devices  31 us (7%)
  matrix products  28.1 us (7%)
  other arithmetic  16.8 us (4%)
  between operations  14.4 us (3%)
    all_to_all x1, waiting for transfers between devices, _finish_screen(): all_to_all(jnp.tile(vec, stack_in), bus_axis, concat_axis=which_dim, tile...  169 us
    all_gather x1, waiting for transfers between devices, per_device(): lax.all_gather(pivot_inverses, 'grp', axis=3, tiled=True)[0]  59.8 us
    all_to_all x1, waiting for transfers between devices, summed_on_arrival(): lax.all_to_all(pieces, axis, split_axis=0, concat_axis=0, tiled=True)  32.4 us
    dot_general x12, matrix products, product(): jnp.dot(first_part, second_part, precision=lax.Precision.HIGHEST, preferr...  28.1 us
    all_to_all x1, starting transfers between devices, per_device(): lax.all_to_all(beta_rows, 'grp', split_axis=2, concat_axis=1, tiled=True)  15.2 us
    ppermute x1, waiting for transfers between devices, partner(): return lax.ppermute(block, axis, route)  12.3 us
    gather x4, local copies, waits for them, and re-layouts, reorder(): return jnp.take(grouped, source, axis=1).reshape(matrix.shape)  11.5 us
    all_to_all x1, starting transfers between devices, _finish_screen(): all_to_all(jnp.tile(vec, stack_in), bus_axis, concat_axis=which_dim, tile...  8.3 us
  transfers between devices with their start and end apart: 5, of which 4 were waited for; matrix products, arithmetic and copies ran while one was open for 4% of the time, Pallas kernels for 0%

profile of v1, /device:TPU:6, one launch (start us, length us, event | category | flops | bytes accessed | tf_op | source)
XLA Modules:
  0.0 413.2 jit_solution(12869813080577825644)
XLA Ops:
  7.2 0.7 all-gather.2.cloned.1.call-update
  7.9 3.5 collective-permute-start
  11.4 12.3 %collective-permute-done = f32[2,64,1024]{2,1,0:T(8,128)S(1)} collective-permute-done((f32[2,64,1024]{2,1,0:T(8,128)}, f32[2,64,1024]{2,1,0:T(8,128)S(1)}, u32[]{:S(2)}, u32[]{:S(2)}) %collective-permute-start) | collective-permute-done | bytes 524320 | tf_op jit(solution)/shard_map/ppermute | solution.py:15
  23.7 1.1 broadcast_select_fusion
  24.8 0.6 copy.46
  25.3 1.9 reshape.141
  27.2 15.2 %all-to-all-start.1 = ((f32[16,1,8192]{2,1,0:T(1,128)}), f32[16,1,8192]{2,1,0:T(1,128)S(1)}, u32[]{:S(2)}, u32[]{:S(2)}) async-start(f32[16,1,8192]{2,1,0:T(1,128)} %reshape.141), calls=%async_computation.1 | async-start | bytes 1048576 | tf_op jit(solution)/shard_map/all_to_all | solution.py:99
  42.5 59.8 %all-gather.2.cloned.1.call-done = f32[1,2,512,512]{2,3,1,0:T(8,128)} async-done(((f32[1,2,512,32]{2,3,1,0:T(8,128)}), f32[1,2,512,512]{2,3,1,0:T(8,128)}) %all-gather.2.cloned.1.call-update) | async-done | bytes 2097168 | tf_op jit(solution)/shard_map/all_gather | solution.py:97
  102.3 2.5 fusion.51
  104.8 2.3 fusion.49
  107.1 1.1 fusion.50
  108.2 1.1 fusion.48
  109.6 3.6 tile.4
  113.2 8.3 %all-to-all-start = ((f32[2,1024,512]{2,0,1:T(2,128)}), f32[2,1024,512]{2,0,1:T(2,128)}, u32[]{:S(2)}, u32[]{:S(2)}) async-start(f32[2,1024,512]{2,0,1:T(2,128)} %bitcast.125), calls=%async_computation | async-start | bytes 8388608 | tf_op jit(solution)/shard_map/all_to_all | solution.py:76
  122.4 1.9 reduce
  124.3 0.8 reshape.142
  125.0 0.6 copy.116
  126.0 0.6 gather_fusion
  126.7 169.4 %all-to-all-done = f32[2,1024,512]{2,0,1:T(2,128)} async-done(((f32[2,1024,512]{2,0,1:T(2,128)}), f32[2,1024,512]{2,0,1:T(2,128)}, u32[]{:S(2)}, u32[]{:S(2)}) %all-to-all-start) | async-done | bytes 4194336 | tf_op jit(solution)/shard_map/all_to_all | solution.py:76
  296.1 7.1 %fusion.62 = (f32[1,1024,512]{2,0,1:T(1,128)S(1)}, f32[1,1024,512]{2,0,1:T(1,128)S(1)}) fusion(f32[2,1024,512]{2,0,1:T(2,128)} %all-to-all-done), kind=kLoop, calls=%fused_computation.88 | loop fusion | bytes 8388608 | tf_op jit(solution)/shard_map/slice | solution.py:49
  303.1 2.2 fusion.6
  305.3 2.2 fusion.4
  307.5 3.7 fusion.2
  311.1 2.4 fusion
  313.5 2.2 fusion.39
  315.7 2.2 fusion.45
  317.8 0.8 maximum_negate_fusion
  318.7 2.2 copy.50
  320.8 4.0 fusion.27
  324.8 2.4 fusion.33
  327.3 1.7 pad_maximum_fusion.1
  329.0 4.5 %copy.51 = f32[2,1024,320]{2,0,1:T(2,128)S(1)} copy(f32[2,1024,320]{1,2,0:T(8,128)} %pad_maximum_fusion.1) | data formatting | bytes 5242880 | tf_op jit(solution)/shard_map/stack | solution.py:51
  333.5 7.7 %pad_maximum_fusion = f32[2,1024,896]{2,0,1:T(2,128)S(1)} fusion(f32[2,1024,320]{2,0,1:T(2,128)S(1)} %copy.51, f32[2,1024,64]{2,0,1:T(2,128)} %copy.50, f32[2,1024,512]{2,0,1:T(2,128)} %all-to-all-done), kind=kLoop, calls=%fused_computation.2 | loop fusion | flops 3670016 | bytes 14680064 | tf_op jit(solution)/shard_map/concatenate | solution.py:104
  341.2 3.4 copy.52
  344.6 7.1 %gather_fusion.1 = f32[8,2,128,896]{3,2,1,0:T(8,128)} fusion(f32[2,8,128,896]{3,2,1,0:T(8,128)} %bitcast.123, s32[1024]{0:T(1024)S(1)} %pad_clamp_fusion), kind=kCustom, calls=%fused_computation.1 | custom fusion | bytes 14680096 | tf_op jit(solution)/shard_map/jit(_take)/gather | solution.py:68
  351.7 3.8 copy.53
  355.5 0.6 bitcast_select_fusion
  356.3 2.2 copy.115
  358.5 1.6 copy-done
  360.1 3.9 all-to-all-start.2
  364.2 2.2 slice-done
  366.4 0.7 constant_dynamic-slice_fusion
  367.1 32.4 %all-to-all-done.2 = f32[2,2,512,384]{3,2,1,0:T(8,128)S(1)} async-done(((f32[2,2,512,384]{3,2,1,0:T(8,128)}), f32[2,2,512,384]{3,2,1,0:T(8,128)S(1)}, u32[]{:S(2)}, u32[]{:S(2)}) %all-to-all-start.2) | async-done | bytes 3145760 | tf_op jit(solution)/shard_map/all_to_all | solution.py:26
  399.5 1.5 reduce_sum.35
  401.0 1.9 split.9
  402.9 1.5 copy.57
  404.4 1.1 slice_add_fusion
  405.5 0.9 copy.56
  (40 shorter events, 1.9 us)
Async XLA Ops:
  7.2 95.1 %all-gather.2.cloned.1.call-start = ((), (), s32[]{:S(2)}) async-start(), calls=%async_computation.3 | async-start | bytes 2228224 | tf_op jit(solution)/shard_map/all_gather | solution.py:97
  7.9 15.8 %collective-permute-start = (f32[2,64,1024]{2,1,0:T(8,128)}, f32[2,64,1024]{2,1,0:T(8,128)S(1)}, u32[]{:S(2)}, u32[]{:S(2)}) collective-permute-start(f32[2,64,1024]{2,1,0:T(8,128)} %bitcast.131), channel_id=1, source_target_pairs={{0,16},{16,0},{1,17},{17,1},{2,18},{18,2},{3,19},{19,3},{4,20},{20... | collective-permute-start | bytes 1572872 | tf_op jit(solution)/shard_map/ppermute | solution.py:15
  24.8 17.7 %copy-start.6 = (f32[1,2,64,1024]{3,2,1,0:T(8,128)S(1)}, f32[1,2,64,1024]{3,2,1,0:T(8,128)}, u32[]{:S(2)}) copy-start(f32[1,2,64,1024]{3,2,1,0:T(8,128)} %param.4) | copy-start | bytes 1572868
  27.2 82.3 %all-to-all-start.1 = ((f32[16,1,8192]{2,1,0:T(1,128)}), f32[16,1,8192]{2,1,0:T(1,128)S(1)}, u32[]{:S(2)}, u32[]{:S(2)}) async-start(f32[16,1,8192]{2,1,0:T(1,128)} %reshape.141), calls=%async_computation.1 | async-start | bytes 1048576 | tf_op jit(solution)/shard_map/all_to_all | solution.py:99
  102.3 4.8 %copy-start.1 = (f32[1,2,512,512]{2,3,1,0:T(8,128)S(1)}, f32[1,2,512,512]{2,3,1,0:T(8,128)}, u32[]{:S(2)}) copy-start(f32[1,2,512,512]{2,3,1,0:T(8,128)} %all-gather.2.cloned.1.call-done) | copy-start | bytes 6291460
  113.2 8.3 %copy-start.7 = (s32[2,8]{1,0:T(2,128)S(1)}, s32[2,8]{1,0:T(2,128)}, u32[]{:S(2)}) copy-start(s32[2,8]{1,0:T(2,128)} %param.7) | copy-start | bytes 196
  113.2 182.9 %all-to-all-start = ((f32[2,1024,512]{2,0,1:T(2,128)}), f32[2,1024,512]{2,0,1:T(2,128)}, u32[]{:S(2)}, u32[]{:S(2)}) async-start(f32[2,1024,512]{2,0,1:T(2,128)} %bitcast.125), calls=%async_computation | async-start | bytes 8388608 | tf_op jit(solution)/shard_map/all_to_all | solution.py:76
  126.7 178.6 %copy-start.4 = (f32[2,512,64]{1,2,0:T(8,128)}, f32[2,512,64]{1,2,0:T(8,128)S(1)}, u32[]{:S(2)}) copy-start(f32[2,512,64]{1,2,0:T(8,128)S(1)} %dynamic-slice_select_fusion) | copy-start | bytes 786436
  303.1 4.3 %copy-start.2 = (f32[2,512,320]{1,2,0:T(8,128)S(1)}, f32[2,512,320]{1,2,0:T(8,128)}, u32[]{:S(2)}) copy-start(f32[2,512,320]{1,2,0:T(8,128)} %param.6) | copy-start | bytes 3932164
  311.1 2.4 copy-start.5
  320.8 4.0 copy-start.3
  356.1 4.0 copy-start
  360.1 39.4 %all-to-all-start.2 = ((f32[2,2,512,384]{3,2,1,0:T(8,128)}), f32[2,2,512,384]{3,2,1,0:T(8,128)S(1)}, u32[]{:S(2)}, u32[]{:S(2)}) async-start(f32[2,2,512,384]{3,2,1,0:T(8,128)} %bitcast.126), calls=%async_computation.2 | async-start | bytes 6291456 | tf_op jit(solution)/shard_map/all_to_all | solution.py:26
  364.2 2.2 slice-start
Sparse Core Ops, SparseCore 0:
  10.1 92.1 all-gather.1
